TPU v7x, 128 devices: a whole 4x4x4 slice. The times are simulated.
128 devices in a mesh: gx: 8 (over y, z_hi), gy: 8 (over x, core), gz: 2 (over z_lo).
Axes of the slice: x: 4, y: 4, z: 4 (z_hi: 2, z_lo: 2; z = z_hi * 2 + z_lo), core: 2. Of those that a mesh axis runs over, the one named last changes fastest.
Arguments:
- density: float32 [32, 256, 256], P('gx', 'gy', 'gz'), may hold values from 0.6 to 1.4
- velocity: float32 [3, 32, 256, 256], P(None, 'gx', 'gy', 'gz'), may hold values from -0.3 to 0.3
- solid_mask: int32 [32, 256, 256], P('gx', 'gy', 'gz'), may hold values 0 or 1
Outputs:
- density_final: float32 [32, 256, 256], P('gx', 'gy', 'gz')
- momentum: float32 [3, 32, 256, 256], P(None, 'gx', 'gy', 'gz')
All inputs are finite; a program needn't handle non-finite values.
Results may differ from a plain program's by a relative error of at most 0.0003.
Values sent between devices are 32-bit elements.
A program may use at most 64 MiB of HBM per device.

v0:
```python
import jax
import jax.numpy as jnp
from jax import lax
from jax.experimental import pallas as pl
from jax.experimental.pallas import tpu as pltpu
from jax.sharding import PartitionSpec as P

MESH = pl.DeviceIdType.MESH

VELOCITIES = [
    (0, 0, 0),
    (1, 0, 0),
    (-1, 0, 0),
    (0, 1, 0),
    (0, -1, 0),
    (0, 0, 1),
    (0, 0, -1),
    (1, 1, 0),
    (-1, -1, 0),
    (1, -1, 0),
    (-1, 1, 0),
    (1, 0, 1),
    (-1, 0, -1),
    (1, 0, -1),
    (-1, 0, 1),
    (0, 1, 1),
    (0, -1, -1),
    (0, 1, -1),
    (0, -1, 1),
]
RELAX_RATE = 1.25
W0, W1, W2 = 1.0 / 3.0, 1.0 / 18.0, 1.0 / 36.0

G = 4
LAYERS, ROWS, LANES = 12, 48, 128
BLOCKS = [4 + 8 * j for j in range(5)]
INNER = [8 + 8 * j for j in range(4)]


def moments(f):
    s = [f[2 * k + 1] + f[2 * k + 2] for k in range(9)]
    d = [f[2 * k + 1] - f[2 * k + 2] for k in range(9)]
    rho = f[0] + (((s[0] + s[1]) + (s[2] + s[3])) + ((s[4] + s[5]) + (s[6] + s[7]))) + s[8]
    mx = d[0] + (d[3] + d[4]) + (d[5] + d[6])
    my = d[1] + (d[3] - d[4]) + (d[7] + d[8])
    mz = d[2] + (d[5] - d[6]) + (d[7] - d[8])
    return rho, mx, my, mz


def balance(rho, m, u, scale):
    mx, my, mz = m
    ux, uy, uz = u
    xx, yy, zz = mx * ux, my * uy, mz * uz
    base = rho - 1.5 * (xx + yy + zz)
    rest = (scale * W0) * base
    b1 = (scale * W1) * base
    b2 = (scale * W2) * base
    k1 = scale * W1 * 4.5
    k2 = scale * W2 * 4.5
    o1 = scale * W1 * 3.0
    o2 = scale * W2 * 3.0
    pairs = [(b1 + k1 * xx, o1 * mx), (b1 + k1 * yy, o1 * my), (b1 + k1 * zz, o1 * mz)]
    px, py, pz = o2 * mx, o2 * my, o2 * mz
    exx, eyy, ezz = k2 * xx, k2 * yy, k2 * zz
    cross_x, cross_y = (2.0 * k2) * mx, (2.0 * k2) * my
    for ea, eb, cross, pa, pb in (
        (exx, eyy, cross_x * uy, px, py),
        (exx, ezz, cross_x * uz, px, pz),
        (eyy, ezz, cross_y * uz, py, pz),
    ):
        even = b2 + (ea + eb)
        pairs.append((even + cross, pa + pb))
        pairs.append((even - cross, pa - pb))
    return rest, pairs


def first(rho, vx, vy, vz, solid):
    sign = jnp.where(solid, -1.0, 1.0)
    u = (vx * sign, vy * sign, vz * sign)
    m = tuple(rho * v for v in u)
    rest, pairs = balance(rho, m, u, 1.0)
    out = [rest]
    for even, odd in pairs:
        out += [even + odd, even - odd]
    return out


def collide(f, solid):
    rho, mx, my, mz = moments(f)
    inv = 1.0 / rho
    rest, pairs = balance(rho, (mx, my, mz), (mx * inv, my * inv, mz * inv), RELAX_RATE)
    keep = 1.0 - RELAX_RATE
    out = [jnp.where(solid, f[0], keep * f[0] + rest)]
    for k, (even, odd) in enumerate(pairs):
        a, b = f[2 * k + 1], f[2 * k + 2]
        out.append(jnp.where(solid, b, keep * a + (even + odd)))
        out.append(jnp.where(solid, a, keep * b + (even - odd)))
    return out


def kernel(
    density,
    velocity,
    mask,
    out_density,
    out_momentum,
    fld,
    msk,
    pack,
    peer,
    gfld,
    gmsk,
    main_a,
    main_b,
    side_a,
    side_b,
    load_sem,
    y_send,
    y_recv,
    z_send,
    z_recv,
    x_send,
    x_recv,
    f_send,
    f_recv,
):
    gx, gy, gz = lax.axis_index("gx"), lax.axis_index("gy"), lax.axis_index("gz")
    par = lax.rem(gx, 2)
    y_up = (gx, lax.rem(gy + 1, 8), gz)
    y_down = (gx, lax.rem(gy + 7, 8), gz)
    z_peer = (gx, gy, 1 - gz)
    x_peer = (gx + 1 - 2 * par, gy, gz)
    fwd_to = (lax.rem(gx + 2 + 4 * par, 8), gy, gz)
    fwd_from = (lax.rem(gx + 6 - 4 * par, 8), gy, gz)

    loads = [
        pltpu.make_async_copy(density, fld.at[0, 4:8, 8:40], load_sem.at[0]),
        pltpu.make_async_copy(velocity, fld.at[1:4, 4:8, 8:40], load_sem.at[1]),
        pltpu.make_async_copy(mask, msk.at[4:8, 8:40], load_sem.at[2]),
    ]
    for c in loads:
        c.start()

    barrier = pltpu.get_barrier_semaphore()
    for dev in (y_up, y_down, z_peer, x_peer, fwd_to, fwd_from):
        pl.semaphore_signal(barrier, inc=1, device_id=dev, device_id_type=MESH)
    pl.semaphore_wait(barrier, 6)
    for c in loads:
        c.wait()

    def remote(src, dst, send, recv, dev):
        return pltpu.make_async_remote_copy(
            src_ref=src, dst_ref=dst, send_sem=send, recv_sem=recv, device_id=dev, device_id_type=MESH
        )

    y_copies = [
        remote(fld.at[:, 4:8, 36:40], fld.at[:, 4:8, 4:8], y_send.at[0], y_recv.at[0], y_up),
        remote(fld.at[:, 4:8, 8:12], fld.at[:, 4:8, 40:44], y_send.at[1], y_recv.at[1], y_down),
        remote(msk.at[4:8, 36:40], msk.at[4:8, 4:8], y_send.at[2], y_recv.at[2], y_up),
        remote(msk.at[4:8, 8:12], msk.at[4:8, 40:44], y_send.at[3], y_recv.at[3], y_down),
    ]
    for c in y_copies:
        c.start()

    near = pl.ds(8 * (1 - par), 4)
    far = pl.ds(8 * par, 4)
    near_slot, far_slot = 2 * (1 - par), 2 * par

    def parts(layers, slot):
        refs = [fld.at[f, layers, 8:40] for f in range(4)] + [msk.at[layers, 8:40]]
        refs += [fld.at[:, layers, 4:8], fld.at[:, layers, 40:44], msk.at[layers, 4:8], msk.at[layers, 40:44]]
        refs += [peer.at[slot, :, 4:44]]
        return refs

    own = pl.ds(4, 4)
    x_copies = [
        remote(a, b, x_send.at[i], x_recv.at[i], x_peer)
        for i, (a, b) in enumerate(zip(parts(own, 1), parts(far, far_slot)))
    ]
    f_copies = [
        remote(a, b, f_send.at[i], f_recv.at[i], fwd_to)
        for i, (a, b) in enumerate(zip(parts(near, near_slot), parts(far, far_slot)))
    ]
    for c in x_copies[:5]:
        c.start()
    for c in y_copies:
        c.wait_recv()
    for c in x_copies[5:9]:
        c.start()

    lane = lax.broadcasted_iota(jnp.int32, (8, LANES), 1)
    group = lane // 8
    low_half = lax.rem(lane, 8) < 4

    for r in BLOCKS:
        rows = slice(r, r + 8)
        acc = None
        for f in range(4):
            for x in range(4):
                part = pltpu.roll(fld[f, 4 + x, rows], 32 * f + 8 * x + 4, 1)
                acc = part if acc is None else jnp.where(group == 4 * f + x, part, acc)
        pack[0, rows] = acc
        acc = None
        for x in range(4):
            part = pltpu.roll(msk[4 + x, rows].astype(jnp.float32), 8 * x + 4, 1)
            acc = part if acc is None else jnp.where(group == x, part, acc)
        pack[1, rows] = acc

    z_copy = remote(pack.at[:, 4:44], peer.at[1, :, 4:44], z_send, z_recv, z_peer)
    x_copies[0].wait_recv()
    f_copies[0].start()
    z_copy.start()
    z_copy.wait_recv()
    x_copies[9].start()
    for i in range(1, 10):
        x_copies[i].wait_recv()
        f_copies[i].start()
    for c in f_copies:
        c.wait_recv()

    def build_side(field, slot_part, slot_shift, store):
        for r in BLOCKS:
            rows = slice(r, r + 8)
            mine = None
            for x in range(LAYERS):
                part = pltpu.roll(field(x, rows), 8 * x + 4, 1)
                mine = part if mine is None else jnp.where(group == x, part, mine)
            theirs = None
            for s in range(3):
                shift = (32 * s - slot_shift) % LANES
                part = peer[s, slot_part, rows]
                part = pltpu.roll(part, shift, 1) if shift else part
                theirs = part if theirs is None else jnp.where(lane // 32 == s, part, theirs)
            store(r, jnp.where(low_half, theirs, mine))
            store(ROWS + r, jnp.where(low_half, mine, theirs))

    for f in range(4):

        def store(r, value, f=f):
            gfld[f, r : r + 8] = value

        build_side(lambda x, rows, f=f: fld[f, x, rows], 0, 32 * f, store)

    def store_mask(r, value):
        gmsk[r : r + 8] = value

    build_side(lambda x, rows: msk[x, rows].astype(jnp.float32), 1, 0, store_mask)

    def first_main(x, carry):
        for r in BLOCKS:
            rows = slice(r, r + 8)
            out = first(fld[0, x, rows], fld[1, x, rows], fld[2, x, rows], fld[3, x, rows], msk[x, rows] == 1)
            for q in range(19):
                main_a[q, x, rows] = out[q]
        return carry

    lax.fori_loop(0, LAYERS, first_main, 0)

    def first_side(i, carry):
        base = i * ROWS
        for r in BLOCKS:
            rows = pl.ds(base + r, 8)
            out = first(gfld[0, rows], gfld[1, rows], gfld[2, rows], gfld[3, rows], gmsk[rows] > 0.5)
            for q in range(19):
                side_a[q, rows] = out[q]
        return carry

    lax.fori_loop(0, 2, first_side, 0)

    def pull_main(main, side, x, r):
        f = []
        for q, (cx, cy, cz) in enumerate(VELOCITIES):
            value = main[q, x - cx, r - cy : r - cy + 8]
            if cz == 1:
                edge = pltpu.roll(side[q, r - cy : r - cy + 8], 125 - 8 * (x - cx), 1)
                value = jnp.where(lane == 0, edge, pltpu.roll(value, 1, 1))
            elif cz == -1:
                edge = pltpu.roll(side[q, ROWS + r - cy : ROWS + r - cy + 8], 123 - 8 * (x - cx), 1)
                value = jnp.where(lane == LANES - 1, edge, pltpu.roll(value, LANES - 1, 1))
            f.append(value)
        return f

    def pull_side(side, base, r):
        f = []
        for q, (cx, cy, cz) in enumerate(VELOCITIES):
            value = side[q, pl.ds(base + r - cy, 8)]
            shift = (8 * cx + cz) % LANES
            f.append(pltpu.roll(value, shift, 1) if shift else value)
        return f

    main, side, main_to, side_to = main_a, side_a, main_b, side_b
    for step in range(1, 4):

        def step_main(x, carry, main=main, side=side, main_to=main_to):
            for r in BLOCKS:
                rows = slice(r, r + 8)
                out = collide(pull_main(main, side, x, r), msk[x, rows] == 1)
                for q in range(19):
                    main_to[q, x, rows] = out[q]
            return carry

        def step_side(i, carry, side=side, side_to=side_to):
            base = i * ROWS
            for r in BLOCKS:
                rows = pl.ds(base + r, 8)
                out = collide(pull_side(side, base, r), gmsk[rows] > 0.5)
                for q in range(19):
                    side_to[q, rows] = out[q]
            return carry

        lax.fori_loop(step, LAYERS - step, step_main, 0)
        lax.fori_loop(0, 2, step_side, 0)
        main, side, main_to, side_to = main_to, side_to, main, side

    def last(x, carry):
        for r in INNER:
            rho, mx, my, mz = moments(pull_main(main, side, x, r))
            rows = slice(r - 8, r)
            out_density[x - 4, rows] = rho
            out_momentum[0, x - 4, rows] = mx
            out_momentum[1, x - 4, rows] = my
            out_momentum[2, x - 4, rows] = mz
        return carry

    lax.fori_loop(4, 8, last, 0)

    for c in y_copies + [z_copy] + x_copies + f_copies:
        c.wait_send()


def local(density, velocity, solid_mask):
    shape = density.shape
    f32 = jnp.float32
    dma = pltpu.SemaphoreType.DMA
    return tuple(
        pl.pallas_call(
            kernel,
            out_shape=(jax.ShapeDtypeStruct(shape, f32), jax.ShapeDtypeStruct((3,) + shape, f32)),
            in_specs=[pl.BlockSpec(memory_space=pl.ANY)] * 3,
            out_specs=(pl.BlockSpec(memory_space=pltpu.VMEM), pl.BlockSpec(memory_space=pltpu.VMEM)),
            scratch_shapes=[
                pltpu.VMEM((4, LAYERS, ROWS, LANES), f32),
                pltpu.VMEM((LAYERS, ROWS, LANES), jnp.int32),
                pltpu.VMEM((2, ROWS, LANES), f32),
                pltpu.VMEM((3, 2, ROWS, LANES), f32),
                pltpu.VMEM((4, 2 * ROWS, LANES), f32),
                pltpu.VMEM((2 * ROWS, LANES), f32),
                pltpu.VMEM((19, LAYERS, ROWS, LANES), f32),
                pltpu.VMEM((19, LAYERS, ROWS, LANES), f32),
                pltpu.VMEM((19, 2 * ROWS, LANES), f32),
                pltpu.VMEM((19, 2 * ROWS, LANES), f32),
                dma((3,)),
                dma((4,)),
                dma((4,)),
                dma,
                dma,
                dma((10,)),
                dma((10,)),
                dma((10,)),
                dma((10,)),
            ],
            compiler_params=pltpu.CompilerParams(collective_id=0, has_side_effects=True, vmem_limit_bytes=48 << 20),
        )(density, velocity, solid_mask)
    )


def solution(mesh):
    return jax.shard_map(
        local,
        mesh=mesh,
        in_specs=(P("gx", "gy", "gz"), P(None, "gx", "gy", "gz"), P("gx", "gy", "gz")),
        out_specs=(P("gx", "gy", "gz"), P(None, "gx", "gy", "gz")),
        check_vma=False,
    )
```

profile of v0, /device:TPU:0, one launch (start us, length us, event | category | flops | bytes accessed | tf_op | source)
XLA Modules:
  0.0 41.0 jit_solution(8580890132661449395)
XLA Ops:
  0.6 0.0 copy-start
  0.6 0.9 %copy-done = f32[3,4,32,128]{3,2,1,0:T(8,128)S(1)} copy-done((f32[3,4,32,128]{3,2,1,0:T(8,128)S(1)}, f32[3,4,32,128]{3,2,1,0:T(8,128)}, u32[]{:S(2)}) %copy-start) | copy-done | bytes 196632
  1.6 0.0 copy-start.1
  1.6 0.8 %copy-done.1 = f32[4,32,128]{2,1,0:T(8,128)S(1)} copy-done((f32[4,32,128]{2,1,0:T(8,128)S(1)}, f32[4,32,128]{2,1,0:T(8,128)}, u32[]{:S(2)}) %copy-start.1) | copy-done | bytes 65560
  2.4 0.0 copy-start.2
  2.4 0.8 %copy-done.2 = s32[4,32,128]{2,1,0:T(8,128)S(1)} copy-done((s32[4,32,128]{2,1,0:T(8,128)S(1)}, s32[4,32,128]{2,1,0:T(8,128)}, u32[]{:S(2)}) %copy-start.2) | copy-done | bytes 65560
  3.2 36.5 %shard_map.50 = (f32[4,32,128]{2,1,0:T(8,128)S(1)}, f32[3,4,32,128]{3,2,1,0:T(8,128)S(1)}) custom-call(f32[4,32,128]{2,1,0:T(8,128)S(1)} %copy-done.1, f32[3,4,32,128]{3,2,1,0:T(8,128)S(1)} %copy-done, s32[4,32,128]{2,1,0:T(8,128)S(1)} %copy-done.2), custom_call_target="tpu_custom_call" | custom-call | tf_op jit(solution)/shard_map/pallas_call | solution.py:336
  39.7 0.6 %copy.7 = f32[4,32,128]{2,1,0:T(8,128)} copy(f32[4,32,128]{2,1,0:T(8,128)S(1)} %get-tuple-element.4) | data formatting | bytes 131072
  40.3 0.7 %copy.8 = f32[3,4,32,128]{3,2,1,0:T(8,128)} copy(f32[3,4,32,128]{3,2,1,0:T(8,128)S(1)} %get-tuple-element.5) | data formatting | bytes 393216
Async XLA Ops:
  0.6 0.9 %copy-start = (f32[3,4,32,128]{3,2,1,0:T(8,128)S(1)}, f32[3,4,32,128]{3,2,1,0:T(8,128)}, u32[]{:S(2)}) copy-start(f32[3,4,32,128]{3,2,1,0:T(8,128)} %velocity.1) | copy-start | bytes 589828
  1.6 0.8 %copy-start.1 = (f32[4,32,128]{2,1,0:T(8,128)S(1)}, f32[4,32,128]{2,1,0:T(8,128)}, u32[]{:S(2)}) copy-start(f32[4,32,128]{2,1,0:T(8,128)} %density.1) | copy-start | bytes 196612
  2.4 0.8 %copy-start.2 = (s32[4,32,128]{2,1,0:T(8,128)S(1)}, s32[4,32,128]{2,1,0:T(8,128)}, u32[]{:S(2)}) copy-start(s32[4,32,128]{2,1,0:T(8,128)} %mask.1) | copy-start | bytes 196612
where the time goes:
time: 41.2 us; the launch traced here: 41 us
  Pallas kernels  36.5 us (89%)
  local copies, waits for them, and re-layouts  3.91 us (9%)
  between operations  0.65 us (2%)
    pallas_call x1, Pallas kernels, local(): pl.pallas_call(kernel, out_shape=(jax.ShapeDtypeStruct(shape, f32), jax.S...  36.5 us
    unnamed x8, local copies, waits for them, and re-layouts  3.91 us

commit v1 on v0

--- a/solution.py
+++ b/solution.py
@@ -44,41 +44,33 @@
     mx = d[0] + (d[3] + d[4]) + (d[5] + d[6])
     my = d[1] + (d[3] - d[4]) + (d[7] + d[8])
     mz = d[2] + (d[5] - d[6]) + (d[7] - d[8])
-    return rho, mx, my, mz
+    return rho, (mx, my, mz), s, d
 
 
 def balance(rho, m, u, scale):
     mx, my, mz = m
     ux, uy, uz = u
     xx, yy, zz = mx * ux, my * uy, mz * uz
-    base = rho - 1.5 * (xx + yy + zz)
-    rest = (scale * W0) * base
-    b1 = (scale * W1) * base
-    b2 = (scale * W2) * base
-    k1 = scale * W1 * 4.5
-    k2 = scale * W2 * 4.5
-    o1 = scale * W1 * 3.0
-    o2 = scale * W2 * 3.0
-    pairs = [(b1 + k1 * xx, o1 * mx), (b1 + k1 * yy, o1 * my), (b1 + k1 * zz, o1 * mz)]
-    px, py, pz = o2 * mx, o2 * my, o2 * mz
-    exx, eyy, ezz = k2 * xx, k2 * yy, k2 * zz
-    cross_x, cross_y = (2.0 * k2) * mx, (2.0 * k2) * my
-    for ea, eb, cross, pa, pb in (
-        (exx, eyy, cross_x * uy, px, py),
-        (exx, ezz, cross_x * uz, px, pz),
-        (eyy, ezz, cross_y * uz, py, pz),
+    base = (scale * W2) * rho - (1.0 / 3.0) * (xx + yy + zz)
+    px, py, pz = (scale * W2 * 3.0) * mx, (scale * W2 * 3.0) * my, (scale * W2 * 3.0) * mz
+    ax, ay, az = base + xx, base + yy, base + zz
+    pairs = [(ax + ax, px + px), (ay + ay, py + py), (az + az, pz + pz)]
+    mx2, my2 = mx + mx, my + my
+    for even, cross, pa, pb in (
+        (ax + yy, mx2 * uy, px, py),
+        (ax + zz, mx2 * uz, px, pz),
+        (ay + zz, my2 * uz, py, pz),
     ):
-        even = b2 + (ea + eb)
         pairs.append((even + cross, pa + pb))
         pairs.append((even - cross, pa - pb))
-    return rest, pairs
+    return (W0 / W2) * base, pairs
 
 
 def first(rho, vx, vy, vz, solid):
     sign = jnp.where(solid, -1.0, 1.0)
-    u = (vx * sign, vy * sign, vz * sign)
-    m = tuple(rho * v for v in u)
-    rest, pairs = balance(rho, m, u, 1.0)
+    m = tuple((rho * sign) * v for v in (vx, vy, vz))
+    half = jnp.where(solid, -W2 * 4.5, W2 * 4.5)
+    rest, pairs = balance(rho, m, tuple(half * v for v in (vx, vy, vz)), 1.0)
     out = [rest]
     for even, odd in pairs:
         out += [even + odd, even - odd]
@@ -86,15 +78,20 @@
 
 
 def collide(f, solid):
-    rho, mx, my, mz = moments(f)
-    inv = 1.0 / rho
-    rest, pairs = balance(rho, (mx, my, mz), (mx * inv, my * inv, mz * inv), RELAX_RATE)
+    rho, m, s, d = moments(f)
+    inv = (RELAX_RATE * W2 * 4.5) / rho
+    u = tuple(v * inv for v in m)
+    rho, *m = (jnp.where(solid, 0.0, v) for v in (rho, *m))
+    rest, pairs = balance(rho, m, u, RELAX_RATE)
     keep = 1.0 - RELAX_RATE
-    out = [jnp.where(solid, f[0], keep * f[0] + rest)]
+    keep_rest = jnp.where(solid, 1.0, keep)
+    keep_sum = jnp.where(solid, 0.5, 0.5 * keep)
+    keep_diff = jnp.where(solid, -0.5, 0.5 * keep)
+    out = [keep_rest * f[0] + rest]
     for k, (even, odd) in enumerate(pairs):
-        a, b = f[2 * k + 1], f[2 * k + 2]
-        out.append(jnp.where(solid, b, keep * a + (even + odd)))
-        out.append(jnp.where(solid, a, keep * b + (even - odd)))
+        even = even + keep_sum * s[k]
+        odd = odd + keep_diff * d[k]
+        out += [even + odd, even - odd]
     return out
 
 
@@ -206,66 +203,60 @@
             acc = part if acc is None else jnp.where(group == x, part, acc)
         pack[1, rows] = acc
 
-    z_copy = remote(pack.at[:, 4:44], peer.at[1, :, 4:44], z_send, z_recv, z_peer)
-    x_copies[0].wait_recv()
-    f_copies[0].start()
-    z_copy.start()
-    z_copy.wait_recv()
-    x_copies[9].start()
-    for i in range(1, 10):
-        x_copies[i].wait_recv()
-        f_copies[i].start()
-    for c in f_copies:
-        c.wait_recv()
-
-    def build_side(field, slot_part, slot_shift, store):
-        for r in BLOCKS:
-            rows = slice(r, r + 8)
-            mine = None
-            for x in range(LAYERS):
-                part = pltpu.roll(field(x, rows), 8 * x + 4, 1)
-                mine = part if mine is None else jnp.where(group == x, part, mine)
-            theirs = None
-            for s in range(3):
-                shift = (32 * s - slot_shift) % LANES
-                part = peer[s, slot_part, rows]
-                part = pltpu.roll(part, shift, 1) if shift else part
-                theirs = part if theirs is None else jnp.where(lane // 32 == s, part, theirs)
-            store(r, jnp.where(low_half, theirs, mine))
-            store(ROWS + r, jnp.where(low_half, mine, theirs))
-
-    for f in range(4):
-
-        def store(r, value, f=f):
-            gfld[f, r : r + 8] = value
-
-        build_side(lambda x, rows, f=f: fld[f, x, rows], 0, 32 * f, store)
-
-    def store_mask(r, value):
-        gmsk[r : r + 8] = value
-
-    build_side(lambda x, rows: msk[x, rows].astype(jnp.float32), 1, 0, store_mask)
-
-    def first_main(x, carry):
+    def first_layer(x):
         for r in BLOCKS:
             rows = slice(r, r + 8)
             out = first(fld[0, x, rows], fld[1, x, rows], fld[2, x, rows], fld[3, x, rows], msk[x, rows] == 1)
             for q in range(19):
                 main_a[q, x, rows] = out[q]
-        return carry
-
-    lax.fori_loop(0, LAYERS, first_main, 0)
-
-    def first_side(i, carry):
-        base = i * ROWS
-        for r in BLOCKS:
-            rows = pl.ds(base + r, 8)
-            out = first(gfld[0, rows], gfld[1, rows], gfld[2, rows], gfld[3, rows], gmsk[rows] > 0.5)
-            for q in range(19):
-                side_a[q, rows] = out[q]
-        return carry
-
-    lax.fori_loop(0, 2, first_side, 0)
+
+    def first_four(start):
+        def body(i, carry):
+            first_layer(start + 2 * i)
+            first_layer(start + 2 * i + 1)
+            return carry
+
+        lax.fori_loop(0, 2, body, 0)
+
+    def first_side():
+        def body(i, carry):
+            for r in BLOCKS:
+                rows = pl.ds(i * ROWS + r, 8)
+                out = first(gfld[0, rows], gfld[1, rows], gfld[2, rows], gfld[3, rows], gmsk[rows] > 0.5)
+                for q in range(19):
+                    side_a[q, rows] = out[q]
+            return carry
+
+        lax.fori_loop(0, 2, body, 0)
+
+    def build_side(start, count, slots, fresh):
+        for f in range(5):
+            shift_back = 32 * f if f < 4 else 0
+            for r in BLOCKS:
+                rows = slice(r, r + 8)
+                low, high = slice(r, r + 8), slice(ROWS + r, ROWS + r + 8)
+                mine = theirs = None
+                for i in range(count):
+                    x = start + i
+                    part = fld[f, x, rows] if f < 4 else msk[x, rows].astype(jnp.float32)
+                    part = pltpu.roll(part, lax.rem(8 * x + 4, LANES), 1)
+                    mine = part if mine is None else jnp.where(group == x, part, mine)
+                for s in slots:
+                    part = peer[s, f // 4, rows]
+                    part = pltpu.roll(part, lax.rem(32 * s + LANES - shift_back, LANES), 1)
+                    theirs = part if theirs is None else jnp.where(lane // 32 == s, part, theirs)
+                below = jnp.where(low_half, theirs, mine)
+                above = jnp.where(low_half, mine, theirs)
+                if not fresh:
+                    here = lane // 32 == slots[0]
+                    old = (gfld[f, low], gfld[f, high]) if f < 4 else (gmsk[low], gmsk[high])
+                    below, above = jnp.where(here, below, old[0]), jnp.where(here, above, old[1])
+                if f < 4:
+                    gfld[f, low] = below
+                    gfld[f, high] = above
+                else:
+                    gmsk[low] = below
+                    gmsk[high] = above
 
     def pull_main(main, side, x, r):
         f = []
@@ -288,38 +279,77 @@
             f.append(pltpu.roll(value, shift, 1) if shift else value)
         return f
 
-    main, side, main_to, side_to = main_a, side_a, main_b, side_b
-    for step in range(1, 4):
-
-        def step_main(x, carry, main=main, side=side, main_to=main_to):
+    buffers = [(main_a, side_a), (main_b, side_b)]
+
+    def step_layers(step, start, count):
+        (main, side), (main_to, _) = buffers[step % 2], buffers[(step + 1) % 2]
+
+        def body(i, carry):
+            for k in range(2):
+                x = start + 2 * i + k
+                for r in BLOCKS:
+                    rows = slice(r, r + 8)
+                    out = collide(pull_main(main, side, x, r), msk[x, rows] == 1)
+                    for q in range(19):
+                        main_to[q, x, rows] = out[q]
+            return carry
+
+        lax.fori_loop(0, count // 2, body, 0)
+
+    def step_side(step):
+        (_, side), (_, side_to) = buffers[step % 2], buffers[(step + 1) % 2]
+
+        def body(i, carry):
             for r in BLOCKS:
-                rows = slice(r, r + 8)
-                out = collide(pull_main(main, side, x, r), msk[x, rows] == 1)
-                for q in range(19):
-                    main_to[q, x, rows] = out[q]
-            return carry
-
-        def step_side(i, carry, side=side, side_to=side_to):
-            base = i * ROWS
-            for r in BLOCKS:
-                rows = pl.ds(base + r, 8)
-                out = collide(pull_side(side, base, r), gmsk[rows] > 0.5)
+                rows = pl.ds(i * ROWS + r, 8)
+                out = collide(pull_side(side, i * ROWS, r), gmsk[rows] > 0.5)
                 for q in range(19):
                     side_to[q, rows] = out[q]
             return carry
 
-        lax.fori_loop(step, LAYERS - step, step_main, 0)
-        lax.fori_loop(0, 2, step_side, 0)
-        main, side, main_to, side_to = main_to, side_to, main, side
+        lax.fori_loop(0, 2, body, 0)
+
+    first_four(4)
+    z_copy = remote(pack.at[:, 4:44], peer.at[1, :, 4:44], z_send, z_recv, z_peer)
+    z_copy.start()
+    x_copies[0].wait_recv()
+    f_copies[0].start()
+    x_copies[1].wait_recv()
+    f_copies[1].start()
+    z_copy.wait_recv()
+    x_copies[9].start()
+    for i in range(2, 10):
+        x_copies[i].wait_recv()
+        f_copies[i].start()
+
+    build_side(4 - 4 * par, 8, (1 - par, 2 - par), True)
+    first_four(8 - 8 * par)
+    first_side()
+    step_layers(2, 5 - 4 * par, 6)
+    step_side(2)
+    step_layers(3, 6 - 4 * par, 4)
+    step_side(3)
+    step_layers(4, 7 - 4 * par, 2)
+
+    for c in f_copies:
+        c.wait_recv()
+    build_side(8 * par, 4, (2 * par,), False)
+    first_four(8 * par)
+    first_side()
+    step_layers(2, 1 + 6 * par, 4)
+    step_side(2)
+    step_layers(3, 2 + 4 * par, 4)
+    step_side(3)
+    step_layers(4, 3 + 2 * par, 4)
+    step_side(4)
 
     def last(x, carry):
         for r in INNER:
-            rho, mx, my, mz = moments(pull_main(main, side, x, r))
+            rho, m, _, _ = moments(pull_main(main_b, side_b, x, r))
             rows = slice(r - 8, r)
             out_density[x - 4, rows] = rho
-            out_momentum[0, x - 4, rows] = mx
-            out_momentum[1, x - 4, rows] = my
-            out_momentum[2, x - 4, rows] = mz
+            for k in range(3):
+                out_momentum[k, x - 4, rows] = m[k]
         return carry
 
     lax.fori_loop(4, 8, last, 0)
@@ -359,7 +389,7 @@
                 dma((10,)),
                 dma((10,)),
             ],
-            compiler_params=pltpu.CompilerParams(collective_id=0, has_side_effects=True, vmem_limit_bytes=48 << 20),
+            compiler_params=pltpu.CompilerParams(collective_id=0, has_side_effects=True, vmem_limit_bytes=67043328),
         )(density, velocity, solid_mask)
     )
 

time: 41.2 us -> 34.7 us (0.84)
  Pallas kernels: 36.5 us -> 30.8 us
  local copies, waits for them, and re-layouts: 3.91 us -> 3.09 us
    pallas_call x1, Pallas kernels: 36.5 us -> 30.8 us  [local(): pl.pallas_call(kernel, out_shape=(jax.ShapeDtypeStruct(shape, f32), jax.S...]
    unnamed x8 -> x2, local copies, waits for them, and re-layouts: 3.91 us -> 3.09 us
where the time goes in v1:
time: 34.7 us; the launch traced here: 34.5 us
  Pallas kernels  30.8 us (89%)
  local copies, waits for them, and re-layouts  3.09 us (9%)
  between operations  0.64 us (2%)
    pallas_call x1, Pallas kernels, local(): pl.pallas_call(kernel, out_shape=(jax.ShapeDtypeStruct(shape, f32), jax.S...  30.8 us
    unnamed x2, local copies, waits for them, and re-layouts  3.09 us

profile of v1, /device:TPU:0, one launch (start us, length us, event | category | flops | bytes accessed | tf_op | source)
XLA Modules:
  0.0 34.5 jit_solution(12774335606866876047)
XLA Ops:
  0.6 30.8 %shard_map.50 = (f32[4,32,128]{2,1,0:T(8,128)}, f32[3,4,32,128]{3,2,1,0:T(8,128)}) custom-call(f32[4,32,128]{2,1,0:T(8,128)} %density.1, f32[3,4,32,128]{3,2,1,0:T(8,128)} %velocity.1, s32[4,32,128]{2,1,0:T(8,128)} %mask.1), custom_call_target="tpu_custom_call" | custom-call | tf_op jit(solution)/shard_map/pallas_call | solution.py:366
  31.5 1.5 %copy.7 = f32[4,32,128]{2,1,0:T(8,128)} copy(f32[4,32,128]{2,1,0:T(8,128)} %get-tuple-element.4) | data formatting | bytes 131072
  32.9 1.6 %copy.8 = f32[3,4,32,128]{3,2,1,0:T(8,128)} copy(f32[3,4,32,128]{3,2,1,0:T(8,128)} %get-tuple-element.5) | data formatting | bytes 393216

commit v2 on v1

--- a/solution.py
+++ b/solution.py
@@ -99,8 +99,7 @@
     density,
     velocity,
     mask,
-    out_density,
-    out_momentum,
+    out,
     fld,
     msk,
     pack,
@@ -141,55 +140,12 @@
     barrier = pltpu.get_barrier_semaphore()
     for dev in (y_up, y_down, z_peer, x_peer, fwd_to, fwd_from):
         pl.semaphore_signal(barrier, inc=1, device_id=dev, device_id_type=MESH)
-    pl.semaphore_wait(barrier, 6)
-    for c in loads:
-        c.wait()
-
-    def remote(src, dst, send, recv, dev):
-        return pltpu.make_async_remote_copy(
-            src_ref=src, dst_ref=dst, send_sem=send, recv_sem=recv, device_id=dev, device_id_type=MESH
-        )
-
-    y_copies = [
-        remote(fld.at[:, 4:8, 36:40], fld.at[:, 4:8, 4:8], y_send.at[0], y_recv.at[0], y_up),
-        remote(fld.at[:, 4:8, 8:12], fld.at[:, 4:8, 40:44], y_send.at[1], y_recv.at[1], y_down),
-        remote(msk.at[4:8, 36:40], msk.at[4:8, 4:8], y_send.at[2], y_recv.at[2], y_up),
-        remote(msk.at[4:8, 8:12], msk.at[4:8, 40:44], y_send.at[3], y_recv.at[3], y_down),
-    ]
-    for c in y_copies:
-        c.start()
-
-    near = pl.ds(8 * (1 - par), 4)
-    far = pl.ds(8 * par, 4)
-    near_slot, far_slot = 2 * (1 - par), 2 * par
-
-    def parts(layers, slot):
-        refs = [fld.at[f, layers, 8:40] for f in range(4)] + [msk.at[layers, 8:40]]
-        refs += [fld.at[:, layers, 4:8], fld.at[:, layers, 40:44], msk.at[layers, 4:8], msk.at[layers, 40:44]]
-        refs += [peer.at[slot, :, 4:44]]
-        return refs
-
-    own = pl.ds(4, 4)
-    x_copies = [
-        remote(a, b, x_send.at[i], x_recv.at[i], x_peer)
-        for i, (a, b) in enumerate(zip(parts(own, 1), parts(far, far_slot)))
-    ]
-    f_copies = [
-        remote(a, b, f_send.at[i], f_recv.at[i], fwd_to)
-        for i, (a, b) in enumerate(zip(parts(near, near_slot), parts(far, far_slot)))
-    ]
-    for c in x_copies[:5]:
-        c.start()
-    for c in y_copies:
-        c.wait_recv()
-    for c in x_copies[5:9]:
-        c.start()
 
     lane = lax.broadcasted_iota(jnp.int32, (8, LANES), 1)
     group = lane // 8
     low_half = lax.rem(lane, 8) < 4
 
-    for r in BLOCKS:
+    def pack_rows(r):
         rows = slice(r, r + 8)
         acc = None
         for f in range(4):
@@ -202,6 +158,52 @@
             part = pltpu.roll(msk[4 + x, rows].astype(jnp.float32), 8 * x + 4, 1)
             acc = part if acc is None else jnp.where(group == x, part, acc)
         pack[1, rows] = acc
+
+    for c in loads:
+        c.wait()
+    for r in BLOCKS[1:-1]:
+        pack_rows(r)
+    pl.semaphore_wait(barrier, 6)
+
+    def remote(src, dst, send, recv, dev):
+        return pltpu.make_async_remote_copy(
+            src_ref=src, dst_ref=dst, send_sem=send, recv_sem=recv, device_id=dev, device_id_type=MESH
+        )
+
+    y_copies = [
+        remote(fld.at[:, 4:8, 36:40], fld.at[:, 4:8, 4:8], y_send.at[0], y_recv.at[0], y_up),
+        remote(fld.at[:, 4:8, 8:12], fld.at[:, 4:8, 40:44], y_send.at[1], y_recv.at[1], y_down),
+        remote(msk.at[4:8, 36:40], msk.at[4:8, 4:8], y_send.at[2], y_recv.at[2], y_up),
+        remote(msk.at[4:8, 8:12], msk.at[4:8, 40:44], y_send.at[3], y_recv.at[3], y_down),
+    ]
+    for c in y_copies:
+        c.start()
+
+    near = pl.ds(8 * (1 - par), 4)
+    far = pl.ds(8 * par, 4)
+    near_slot, far_slot = 2 * (1 - par), 2 * par
+
+    def parts(layers, slot):
+        refs = [fld.at[f, layers, 8:40] for f in range(4)] + [msk.at[layers, 8:40]]
+        refs += [fld.at[:, layers, 4:8], fld.at[:, layers, 40:44], msk.at[layers, 4:8], msk.at[layers, 40:44]]
+        refs += [peer.at[slot, :, 4:44]]
+        return refs
+
+    own = pl.ds(4, 4)
+    x_copies = [
+        remote(a, b, x_send.at[i], x_recv.at[i], x_peer)
+        for i, (a, b) in enumerate(zip(parts(own, 1), parts(far, far_slot)))
+    ]
+    f_copies = [
+        remote(a, b, f_send.at[i], f_recv.at[i], fwd_to)
+        for i, (a, b) in enumerate(zip(parts(near, near_slot), parts(far, far_slot)))
+    ]
+    for c in x_copies[:4]:
+        c.start()
+    for c in y_copies:
+        c.wait_recv()
+    pack_rows(BLOCKS[0])
+    pack_rows(BLOCKS[-1])
 
     def first_layer(x):
         for r in BLOCKS:
@@ -312,13 +314,16 @@
     first_four(4)
     z_copy = remote(pack.at[:, 4:44], peer.at[1, :, 4:44], z_send, z_recv, z_peer)
     z_copy.start()
+    for c in x_copies[4:9]:
+        c.start()
     x_copies[0].wait_recv()
     f_copies[0].start()
-    x_copies[1].wait_recv()
-    f_copies[1].start()
+    for i in range(1, 4):
+        x_copies[i].wait_recv()
+        f_copies[i].start()
     z_copy.wait_recv()
     x_copies[9].start()
-    for i in range(2, 10):
+    for i in range(4, 10):
         x_copies[i].wait_recv()
         f_copies[i].start()
 
@@ -347,27 +352,36 @@
         for r in INNER:
             rho, m, _, _ = moments(pull_main(main_b, side_b, x, r))
             rows = slice(r - 8, r)
-            out_density[x - 4, rows] = rho
-            for k in range(3):
-                out_momentum[k, x - 4, rows] = m[k]
+            for k, value in enumerate((rho, *m)):
+                out[k, x - 4, rows] = value
         return carry
 
     lax.fori_loop(4, 8, last, 0)
 
     for c in y_copies + [z_copy] + x_copies + f_copies:
         c.wait_send()
+
+
+def split(both, density, momentum, sem):
+    copies = [
+        pltpu.make_async_copy(both.at[0], density, sem.at[0]),
+        pltpu.make_async_copy(both.at[1:4], momentum, sem.at[1]),
+    ]
+    for c in copies:
+        c.start()
+    for c in copies:
+        c.wait()
 
 
 def local(density, velocity, solid_mask):
     shape = density.shape
     f32 = jnp.float32
     dma = pltpu.SemaphoreType.DMA
-    return tuple(
-        pl.pallas_call(
+    both = pl.pallas_call(
             kernel,
-            out_shape=(jax.ShapeDtypeStruct(shape, f32), jax.ShapeDtypeStruct((3,) + shape, f32)),
+            out_shape=jax.ShapeDtypeStruct((4,) + shape, f32),
             in_specs=[pl.BlockSpec(memory_space=pl.ANY)] * 3,
-            out_specs=(pl.BlockSpec(memory_space=pltpu.VMEM), pl.BlockSpec(memory_space=pltpu.VMEM)),
+            out_specs=pl.BlockSpec(memory_space=pltpu.VMEM),
             scratch_shapes=[
                 pltpu.VMEM((4, LAYERS, ROWS, LANES), f32),
                 pltpu.VMEM((LAYERS, ROWS, LANES), jnp.int32),
@@ -389,8 +403,17 @@
                 dma((10,)),
                 dma((10,)),
             ],
-            compiler_params=pltpu.CompilerParams(collective_id=0, has_side_effects=True, vmem_limit_bytes=67043328),
-        )(density, velocity, solid_mask)
+            compiler_params=pltpu.CompilerParams(collective_id=0, has_side_effects=True, vmem_limit_bytes=51043328),
+        )(*[pltpu.with_memory_space_constraint(v, pltpu.HBM) for v in (density, velocity, solid_mask)])
+    return tuple(
+        pl.pallas_call(
+            split,
+            out_shape=(jax.ShapeDtypeStruct(shape, f32), jax.ShapeDtypeStruct((3,) + shape, f32)),
+            in_specs=[pl.BlockSpec(memory_space=pltpu.VMEM)],
+            out_specs=(pl.BlockSpec(memory_space=pl.ANY), pl.BlockSpec(memory_space=pl.ANY)),
+            scratch_shapes=[dma((2,))],
+            compiler_params=pltpu.CompilerParams(vmem_limit_bytes=32 << 20),
+        )(both)
     )
 
 

time: 34.7 us -> 29.6 us (0.85)
  local copies, waits for them, and re-layouts: 3.09 us -> 0 us
  Pallas kernels: 30.8 us -> 28.9 us
    unnamed x2 -> x0, local copies, waits for them, and re-layouts: 3.09 us -> none
    pallas_call x1 -> x2, Pallas kernels: 30.8 us -> 28.9 us  [the longest x1 28.1 us: local(): pl.pallas_call(kernel, out_shape=jax.ShapeDtypeStruct((4,) + shape, f32),...]
where the time goes in v2:
time: 29.6 us; the launch traced here: 29.5 us
  Pallas kernels  28.9 us (98%)
  between operations  0.64 us (2%)
    pallas_call x1, Pallas kernels, local(): pl.pallas_call(kernel, out_shape=jax.ShapeDtypeStruct((4,) + shape, f32),...  28.1 us
    pallas_call x1, Pallas kernels, local(): pl.pallas_call(split, out_shape=(jax.ShapeDtypeStruct(shape, f32), jax.Sh...  0.72 us

profile of v2, /device:TPU:0, one launch (start us, length us, event | category | flops | bytes accessed | tf_op | source)
XLA Modules:
  0.0 29.5 jit_solution(944545409265123721)
XLA Ops:
  0.6 28.1 %shard_map.50.both = f32[4,4,32,128]{3,2,1,0:T(8,128)S(1)} custom-call(f32[4,32,128]{2,1,0:T(8,128)} %density.1, f32[3,4,32,128]{3,2,1,0:T(8,128)} %velocity.1, s32[4,32,128]{2,1,0:T(8,128)} %mask.1), custom_call_target="tpu_custom_call" | custom-call | tf_op jit(solution)/shard_map/pallas_call | solution.py:380
  28.8 0.7 %shard_map.51 = (f32[4,32,128]{2,1,0:T(8,128)}, f32[3,4,32,128]{3,2,1,0:T(8,128)}) custom-call(f32[4,4,32,128]{3,2,1,0:T(8,128)S(1)} %shard_map.50.both), custom_call_target="tpu_custom_call" | custom-call | tf_op jit(solution)/shard_map/pallas_call | solution.py:409

commit v3 on v2

--- a/solution.py
+++ b/solution.py
@@ -119,6 +119,8 @@
     x_recv,
     f_send,
     f_recv,
+    e_send,
+    e_recv,
 ):
     gx, gy, gz = lax.axis_index("gx"), lax.axis_index("gy"), lax.axis_index("gz")
     par = lax.rem(gx, 2)
@@ -185,7 +187,7 @@
 
     def parts(layers, slot):
         refs = [fld.at[f, layers, 8:40] for f in range(4)] + [msk.at[layers, 8:40]]
-        refs += [fld.at[:, layers, 4:8], fld.at[:, layers, 40:44], msk.at[layers, 4:8], msk.at[layers, 40:44]]
+        refs += [fld.at[3, layers, 4:8], fld.at[3, layers, 40:44], msk.at[layers, 4:8], msk.at[layers, 40:44]]
         refs += [peer.at[slot, :, 4:44]]
         return refs
 
@@ -198,7 +200,14 @@
         remote(a, b, f_send.at[i], f_recv.at[i], fwd_to)
         for i, (a, b) in enumerate(zip(parts(near, near_slot), parts(far, far_slot)))
     ]
-    for c in x_copies[:4]:
+    e_copies = []
+    for i, layers in enumerate((near, far)):
+        up, down = fld.at[0:3, layers, 36:40], fld.at[0:3, layers, 8:12]
+        e_copies += [
+            remote(up, fld.at[0:3, layers, 4:8], e_send.at[2 * i], e_recv.at[2 * i], y_up),
+            remote(down, fld.at[0:3, layers, 40:44], e_send.at[2 * i + 1], e_recv.at[2 * i + 1], y_down),
+        ]
+    for c in x_copies[:3]:
         c.start()
     for c in y_copies:
         c.wait_recv()
@@ -286,9 +295,11 @@
     def step_layers(step, start, count):
         (main, side), (main_to, _) = buffers[step % 2], buffers[(step + 1) % 2]
 
+        unroll = 4 if count == 4 else 2
+
         def body(i, carry):
-            for k in range(2):
-                x = start + 2 * i + k
+            for k in range(unroll):
+                x = start + unroll * i + k
                 for r in BLOCKS:
                     rows = slice(r, r + 8)
                     out = collide(pull_main(main, side, x, r), msk[x, rows] == 1)
@@ -296,7 +307,7 @@
                         main_to[q, x, rows] = out[q]
             return carry
 
-        lax.fori_loop(0, count // 2, body, 0)
+        lax.fori_loop(0, count // unroll, body, 0)
 
     def step_side(step):
         (_, side), (_, side_to) = buffers[step % 2], buffers[(step + 1) % 2]
@@ -311,21 +322,29 @@
 
         lax.fori_loop(0, 2, body, 0)
 
-    first_four(4)
     z_copy = remote(pack.at[:, 4:44], peer.at[1, :, 4:44], z_send, z_recv, z_peer)
     z_copy.start()
-    for c in x_copies[4:9]:
-        c.start()
-    x_copies[0].wait_recv()
-    f_copies[0].start()
-    for i in range(1, 4):
+    for c in x_copies[3:9]:
+        c.start()
+    first_four(4)
+    for i in range(3):
         x_copies[i].wait_recv()
         f_copies[i].start()
+    for c in e_copies[:2]:
+        c.start()
     z_copy.wait_recv()
     x_copies[9].start()
+    x_copies[3].wait_recv()
+    f_copies[3].start()
     for i in range(4, 10):
         x_copies[i].wait_recv()
         f_copies[i].start()
+    for c in f_copies[:3]:
+        c.wait_recv()
+    for c in e_copies[2:]:
+        c.start()
+    for c in e_copies[:2]:
+        c.wait_recv()
 
     build_side(4 - 4 * par, 8, (1 - par, 2 - par), True)
     first_four(8 - 8 * par)
@@ -336,7 +355,7 @@
     step_side(3)
     step_layers(4, 7 - 4 * par, 2)
 
-    for c in f_copies:
+    for c in f_copies[3:] + e_copies[2:]:
         c.wait_recv()
     build_side(8 * par, 4, (2 * par,), False)
     first_four(8 * par)
@@ -348,17 +367,17 @@
     step_layers(4, 3 + 2 * par, 4)
     step_side(4)
 
-    def last(x, carry):
+    def last(x):
         for r in INNER:
             rho, m, _, _ = moments(pull_main(main_b, side_b, x, r))
             rows = slice(r - 8, r)
             for k, value in enumerate((rho, *m)):
                 out[k, x - 4, rows] = value
-        return carry
-
-    lax.fori_loop(4, 8, last, 0)
-
-    for c in y_copies + [z_copy] + x_copies + f_copies:
+
+    for x in range(4, 8):
+        last(x)
+
+    for c in y_copies + [z_copy] + x_copies + f_copies + e_copies:
         c.wait_send()
 
 
@@ -402,6 +421,8 @@
                 dma((10,)),
                 dma((10,)),
                 dma((10,)),
+                dma((4,)),
+                dma((4,)),
             ],
             compiler_params=pltpu.CompilerParams(collective_id=0, has_side_effects=True, vmem_limit_bytes=51043328),
         )(*[pltpu.with_memory_space_constraint(v, pltpu.HBM) for v in (density, velocity, solid_mask)])

time: 29.6 us -> 28 us (0.946)
  Pallas kernels: 28.9 us -> 27.1 us
    pallas_call x1, Pallas kernels: 28.1 us -> 26.4 us  [local(): pl.pallas_call(kernel, out_shape=jax.ShapeDtypeStruct((4,) + shape, f32),...]
where the time goes in v3:
time: 28 us; the launch traced here: 27.8 us
  Pallas kernels  27.1 us (97%)
  between operations  0.64 us (2%)
    pallas_call x1, Pallas kernels, local(): pl.pallas_call(kernel, out_shape=jax.ShapeDtypeStruct((4,) + shape, f32),...  26.4 us
    pallas_call x1, Pallas kernels, local(): pl.pallas_call(split, out_shape=(jax.ShapeDtypeStruct(shape, f32), jax.Sh...  0.72 us

profile of v3, /device:TPU:0, one launch (start us, length us, event | category | flops | bytes accessed | tf_op | source)
XLA Modules:
  0.0 27.8 jit_solution(5115760027934916281)
XLA Ops:
  0.6 26.4 %shard_map.50.both = f32[4,4,32,128]{3,2,1,0:T(8,128)S(1)} custom-call(f32[4,32,128]{2,1,0:T(8,128)} %density.1, f32[3,4,32,128]{3,2,1,0:T(8,128)} %velocity.1, s32[4,32,128]{2,1,0:T(8,128)} %mask.1), custom_call_target="tpu_custom_call" | custom-call | tf_op jit(solution)/shard_map/pallas_call | solution.py:399
  27.0 0.7 %shard_map.51 = (f32[4,32,128]{2,1,0:T(8,128)}, f32[3,4,32,128]{3,2,1,0:T(8,128)}) custom-call(f32[4,4,32,128]{3,2,1,0:T(8,128)S(1)} %shard_map.50.both), custom_call_target="tpu_custom_call" | custom-call | tf_op jit(solution)/shard_map/pallas_call | solution.py:430

commit v4 on v3

v4 whole, which is shorter than its diff:
```python
import jax
import jax.numpy as jnp
from jax import lax
from jax.experimental import pallas as pl
from jax.experimental.pallas import tpu as pltpu
from jax.sharding import PartitionSpec as P

MESH = pl.DeviceIdType.MESH

VELOCITIES = [
    (0, 0, 0),
    (1, 0, 0),
    (-1, 0, 0),
    (0, 1, 0),
    (0, -1, 0),
    (0, 0, 1),
    (0, 0, -1),
    (1, 1, 0),
    (-1, -1, 0),
    (1, -1, 0),
    (-1, 1, 0),
    (1, 0, 1),
    (-1, 0, -1),
    (1, 0, -1),
    (-1, 0, 1),
    (0, 1, 1),
    (0, -1, -1),
    (0, 1, -1),
    (0, -1, 1),
]
RELAX_RATE = 1.25
W0, W1, W2 = 1.0 / 3.0, 1.0 / 18.0, 1.0 / 36.0

LAYERS, ROWS, LANES = 12, 48, 128
BLOCKS = [4 + 8 * j for j in range(5)]
SIDE = 4


def moments(f):
    s = [f[2 * k + 1] + f[2 * k + 2] for k in range(9)]
    d = [f[2 * k + 1] - f[2 * k + 2] for k in range(9)]
    rho = f[0] + (((s[0] + s[1]) + (s[2] + s[3])) + ((s[4] + s[5]) + (s[6] + s[7]))) + s[8]
    mx = d[0] + (d[3] + d[4]) + (d[5] + d[6])
    my = d[1] + (d[3] - d[4]) + (d[7] + d[8])
    mz = d[2] + (d[5] - d[6]) + (d[7] - d[8])
    return rho, (mx, my, mz), s, d


def balance(rho, m, u, scale):
    mx, my, mz = m
    ux, uy, uz = u
    xx, yy, zz = mx * ux, my * uy, mz * uz
    base = (scale * W2) * rho - (1.0 / 3.0) * (xx + yy + zz)
    px, py, pz = (scale * W2 * 3.0) * mx, (scale * W2 * 3.0) * my, (scale * W2 * 3.0) * mz
    ax, ay, az = base + xx, base + yy, base + zz
    pairs = [(ax + ax, px + px), (ay + ay, py + py), (az + az, pz + pz)]
    mx2, my2 = mx + mx, my + my
    for even, cross, pa, pb in (
        (ax + yy, mx2 * uy, px, py),
        (ax + zz, mx2 * uz, px, pz),
        (ay + zz, my2 * uz, py, pz),
    ):
        pairs.append((even + cross, pa + pb))
        pairs.append((even - cross, pa - pb))
    return (W0 / W2) * base, pairs


def first(rho, vx, vy, vz, solid):
    sign = jnp.where(solid, -1.0, 1.0)
    m = tuple((rho * sign) * v for v in (vx, vy, vz))
    half = jnp.where(solid, -W2 * 4.5, W2 * 4.5)
    rest, pairs = balance(rho, m, tuple(half * v for v in (vx, vy, vz)), 1.0)
    out = [rest]
    for even, odd in pairs:
        out += [even + odd, even - odd]
    return out


def collide(f, solid):
    rho, m, s, d = moments(f)
    inv = (RELAX_RATE * W2 * 4.5) / rho
    u = tuple(v * inv for v in m)
    rho, *m = (jnp.where(solid, 0.0, v) for v in (rho, *m))
    rest, pairs = balance(rho, m, u, RELAX_RATE)
    keep = 1.0 - RELAX_RATE
    keep_rest = jnp.where(solid, 1.0, keep)
    keep_sum = jnp.where(solid, 0.5, 0.5 * keep)
    keep_diff = jnp.where(solid, -0.5, 0.5 * keep)
    out = [keep_rest * f[0] + rest]
    for k, (even, odd) in enumerate(pairs):
        even = even + keep_sum * s[k]
        odd = odd + keep_diff * d[k]
        out += [even + odd, even - odd]
    return out


def kernel(
    density,
    velocity,
    mask,
    out,
    fld,
    msk,
    pack,
    peer,
    gmsk,
    main_a,
    main_b,
    side_a,
    side_b,
    load_sem,
    y_send,
    y_recv,
    z_send,
    z_recv,
    x_send,
    x_recv,
    f_send,
    f_recv,
    e_send,
    e_recv,
):
    gx, gy, gz = lax.axis_index("gx"), lax.axis_index("gy"), lax.axis_index("gz")
    par = lax.rem(gx, 2)
    y_up = (gx, lax.rem(gy + 1, 8), gz)
    y_down = (gx, lax.rem(gy + 7, 8), gz)
    z_peer = (gx, gy, 1 - gz)
    x_peer = (gx + 1 - 2 * par, gy, gz)
    fwd_to = (lax.rem(gx + 2 + 4 * par, 8), gy, gz)
    fwd_from = (lax.rem(gx + 6 - 4 * par, 8), gy, gz)

    loads = [
        pltpu.make_async_copy(density, fld.at[0, 4:8, 8:40], load_sem.at[0]),
        pltpu.make_async_copy(velocity, fld.at[1:4, 4:8, 8:40], load_sem.at[1]),
        pltpu.make_async_copy(mask, msk.at[4:8, 8:40], load_sem.at[2]),
    ]
    for c in loads:
        c.start()

    barrier = pltpu.get_barrier_semaphore()
    for dev in (y_up, y_down, z_peer, x_peer, fwd_to, fwd_from):
        pl.semaphore_signal(barrier, inc=1, device_id=dev, device_id_type=MESH)

    lane = lax.broadcasted_iota(jnp.int32, (8, LANES), 1)
    group = lane // 8
    low_half = lax.rem(lane, 8) < 4

    def field_rows(f, x, r):
        return fld[f, x, r : r + 8] if f < 4 else msk[x, r : r + 8].astype(jnp.float32)

    def columns(f, x):
        acc = None
        for b, r in enumerate(BLOCKS):
            part = pltpu.roll(field_rows(f, x, r), 8 * b + 4, 1)
            acc = part if acc is None else jnp.where(group == b, part, acc)
        return acc

    for c in loads:
        c.wait()
    pl.semaphore_wait(barrier, 6)

    def remote(src, dst, send, recv, dev):
        return pltpu.make_async_remote_copy(
            src_ref=src, dst_ref=dst, send_sem=send, recv_sem=recv, device_id=dev, device_id_type=MESH
        )

    y_copies = [
        remote(fld.at[:, 4:8, 36:40], fld.at[:, 4:8, 4:8], y_send.at[0], y_recv.at[0], y_up),
        remote(fld.at[:, 4:8, 8:12], fld.at[:, 4:8, 40:44], y_send.at[1], y_recv.at[1], y_down),
        remote(msk.at[4:8, 36:40], msk.at[4:8, 4:8], y_send.at[2], y_recv.at[2], y_up),
        remote(msk.at[4:8, 8:12], msk.at[4:8, 40:44], y_send.at[3], y_recv.at[3], y_down),
    ]
    for c in y_copies:
        c.start()

    near = 8 * (1 - par)
    far = 8 * par
    near_slot, far_slot = 2 * (1 - par), 2 * par

    def parts(start, slot):
        layers = pl.ds(start, 4)
        refs = [fld.at[f, layers, 8:40] for f in range(3)]
        refs += [fld.at[3, layers, 4:44], msk.at[pl.ds(start, 2), 4:44], msk.at[pl.ds(start + 2, 2), 4:44]]
        refs += [peer.at[slot]]
        return refs

    x_copies = [
        remote(a, b, x_send.at[i], x_recv.at[i], x_peer)
        for i, (a, b) in enumerate(zip(parts(4, 1), parts(far, far_slot)))
    ]
    f_copies = [
        remote(a, b, f_send.at[i], f_recv.at[i], fwd_to)
        for i, (a, b) in enumerate(zip(parts(near, near_slot), parts(far, far_slot)))
    ]
    e_copies = []
    for i, layers in enumerate((pl.ds(near, 4), pl.ds(far, 4))):
        up, down = fld.at[0:3, layers, 36:40], fld.at[0:3, layers, 8:12]
        e_copies += [
            remote(up, fld.at[0:3, layers, 4:8], e_send.at[2 * i], e_recv.at[2 * i], y_up),
            remote(down, fld.at[0:3, layers, 40:44], e_send.at[2 * i + 1], e_recv.at[2 * i + 1], y_down),
        ]
    for c in x_copies[:3]:
        c.start()
    for c in y_copies:
        c.wait_recv()
    for v in range(7):
        acc = None
        for k, m in enumerate(range(3 * v, min(3 * v + 3, 20))):
            part = columns(m // 4, 4 + m % 4)
            part = pltpu.roll(part, 40 * k, 1) if k else part
            acc = part if acc is None else jnp.where(group >= 5 * k, part, acc)
        pack[v] = acc

    def first_four(start):
        def body(i, carry):
            for x in (start + 2 * i, start + 2 * i + 1):
                for r in BLOCKS:
                    rows = slice(r, r + 8)
                    out = first(fld[0, x, rows], fld[1, x, rows], fld[2, x, rows], fld[3, x, rows], msk[x, rows] == 1)
                    for q in range(19):
                        main_a[q, x, rows] = out[q]
            return carry

        lax.fori_loop(0, 2, body, 0)

    def store_side(side, x, out):
        for q, (_, cy, _) in enumerate(VELOCITIES):
            side[q, x, SIDE : SIDE + 8] = out[q]
            if cy == 1:
                side[q, x, SIDE - 1 : SIDE] = pltpu.roll(out[q], 8, 1)[7:8]
            elif cy == -1:
                side[q, x, SIDE + 8 : SIDE + 9] = pltpu.roll(out[q], LANES - 8, 1)[0:1]

    def first_side(start, slot):
        for i in range(4):
            x = start + i
            cells = []
            for f in range(5):
                m = 4 * f + i
                mine = columns(f, x)
                theirs = peer[slot, m // 3]
                theirs = pltpu.roll(theirs, LANES - 40 * (m % 3), 1) if m % 3 else theirs
                above = pltpu.roll(jnp.where(low_half, mine, theirs), 64, 1)
                cells.append(jnp.where(lane < 64, jnp.where(low_half, theirs, mine), above))
            gmsk[x] = cells[4]
            store_side(side_a, x, first(*cells[:4], cells[4] > 0.5))

    def pull_main(main, side, x, b):
        f = []
        r = BLOCKS[b]
        for q, (cx, cy, cz) in enumerate(VELOCITIES):
            value = main[q, x - cx, r - cy : r - cy + 8]
            if cz:
                edge = side[q, x - cx, SIDE - cy : SIDE - cy + 8]
                if cz == 1:
                    edge = pltpu.roll(edge, (125 - 8 * b) % LANES, 1)
                    value = jnp.where(lane == 0, edge, pltpu.roll(value, 1, 1))
                else:
                    edge = pltpu.roll(edge, 59 - 8 * b, 1)
                    value = jnp.where(lane == LANES - 1, edge, pltpu.roll(value, LANES - 1, 1))
            f.append(value)
        return f

    def pull_side(side, x):
        f = []
        for q, (cx, cy, cz) in enumerate(VELOCITIES):
            value = side[q, x - cx, SIDE - cy : SIDE - cy + 8]
            f.append(pltpu.roll(value, cz % LANES, 1) if cz else value)
        return f

    buffers = [(main_a, side_a), (main_b, side_b)]

    def step_layers(step, start, count):
        (main, side), (main_to, side_to) = buffers[step % 2], buffers[(step + 1) % 2]
        unroll = 2

        def body(i, carry):
            for k in range(unroll):
                x = start + unroll * i + k
                store_side(side_to, x, collide(pull_side(side, x), gmsk[x] > 0.5))
            for k in range(unroll):
                x = start + unroll * i + k
                for b, r in enumerate(BLOCKS):
                    rows = slice(r, r + 8)
                    out = collide(pull_main(main, side, x, b), msk[x, rows] == 1)
                    for q in range(19):
                        main_to[q, x, rows] = out[q]
            return carry

        lax.fori_loop(0, count // unroll, body, 0)

    z_copy = remote(pack, peer.at[1], z_send, z_recv, z_peer)
    z_copy.start()
    for c in x_copies[3:6]:
        c.start()
    first_four(4)
    for i in range(3):
        x_copies[i].wait_recv()
        f_copies[i].start()
    for c in e_copies[:2]:
        c.start()
    z_copy.wait_recv()
    x_copies[6].start()
    x_copies[3].wait_recv()
    f_copies[3].start()
    for i in range(4, 7):
        x_copies[i].wait_recv()
        f_copies[i].start()
    for c in f_copies[:3]:
        c.wait_recv()
    for c in e_copies[2:]:
        c.start()
    for c in e_copies[:2]:
        c.wait_recv()

    first_side(4, 1)
    first_four(8 - 8 * par)
    first_side(8 - 8 * par, near_slot)
    step_layers(2, 5 - 4 * par, 6)
    step_layers(3, 6 - 4 * par, 4)
    step_layers(4, 7 - 4 * par, 2)

    for c in f_copies[3:] + e_copies[2:]:
        c.wait_recv()
    first_four(8 * par)
    first_side(8 * par, far_slot)
    step_layers(2, 1 + 6 * par, 4)
    step_layers(3, 2 + 4 * par, 4)
    step_layers(4, 3 + 2 * par, 4)

    def pull(ref, x, row, cz):
        part = {c[:2]: ref[q, x - c[0], row - c[1] : row - c[1] + 8] for q, c in enumerate(VELOCITIES) if c[2] == cz}
        sums = [part[0, 0], part[1, 0] - part[-1, 0], part[0, 1] - part[0, -1]]
        sums[0] += (part[1, 0] + part[-1, 0]) + (part[0, 1] + part[0, -1])
        if not cz:
            diagonal = [part[1, 1], part[-1, -1], part[1, -1], part[-1, 1]]
            sums[0] += (diagonal[0] + diagonal[1]) + (diagonal[2] + diagonal[3])
            sums[1] += (diagonal[0] - diagonal[1]) + (diagonal[2] - diagonal[3])
            sums[2] += (diagonal[0] - diagonal[1]) - (diagonal[2] - diagonal[3])
        return sums

    def moved(x, b, cz):
        row = BLOCKS[b]
        shift, edge_lane = ((125 - 8 * b) % LANES, 0) if cz == 1 else (59 - 8 * b, LANES - 1)
        result = []
        for value, edge in zip(pull(main_b, x, row, cz), pull(side_b, x, SIDE, cz)):
            value = pltpu.roll(value, cz % LANES, 1)
            result.append(jnp.where(lane == edge_lane, pltpu.roll(edge, shift, 1), value))
        return result

    def last(i, carry):
        for x in [4 + 4 * i + k for k in range(4)]:
            for b, r in enumerate(BLOCKS):
                rest, up, down = pull(main_b, x, r, 0), moved(x, b, 1), moved(x, b, -1)
                rho, mx, my = (rest[k] + (up[k] + down[k]) for k in range(3))
                low, high = max(r, 8), min(r + 8, 40)
                for k, value in enumerate((rho, mx, my, up[0] - down[0])):
                    out[k, x - 4, low - 8 : high - 8] = value[low - r : high - r]
        return carry

    lax.fori_loop(0, 4 // 4, last, 0)

    for c in y_copies + [z_copy] + x_copies + f_copies + e_copies:
        c.wait_send()


def split(both, density, momentum, sem):
    copies = [
        pltpu.make_async_copy(both.at[0], density, sem.at[0]),
        pltpu.make_async_copy(both.at[1:4], momentum, sem.at[1]),
    ]
    for c in copies:
        c.start()
    for c in copies:
        c.wait()


def local(density, velocity, solid_mask):
    shape = density.shape
    f32 = jnp.float32
    dma = pltpu.SemaphoreType.DMA
    both = pl.pallas_call(
            kernel,
            out_shape=jax.ShapeDtypeStruct((4,) + shape, f32),
            in_specs=[pl.BlockSpec(memory_space=pl.ANY)] * 3,
            out_specs=pl.BlockSpec(memory_space=pltpu.VMEM),
            scratch_shapes=[
                pltpu.VMEM((4, LAYERS, ROWS, LANES), f32),
                pltpu.VMEM((LAYERS, ROWS, LANES), jnp.int32),
                pltpu.VMEM((7, 8, LANES), f32),
                pltpu.VMEM((3, 7, 8, LANES), f32),
                pltpu.VMEM((LAYERS, 8, LANES), f32),
                pltpu.VMEM((19, LAYERS, ROWS, LANES), f32),
                pltpu.VMEM((19, LAYERS, ROWS, LANES), f32),
                pltpu.VMEM((19, LAYERS, 16, LANES), f32),
                pltpu.VMEM((19, LAYERS, 16, LANES), f32),
                dma((3,)),
                dma((4,)),
                dma((4,)),
                dma,
                dma,
                dma((7,)),
                dma((7,)),
                dma((7,)),
                dma((7,)),
                dma((4,)),
                dma((4,)),
            ],
            compiler_params=pltpu.CompilerParams(collective_id=0, has_side_effects=True, vmem_limit_bytes=51043328),
        )(*[pltpu.with_memory_space_constraint(v, pltpu.HBM) for v in (density, velocity, solid_mask)])
    return tuple(
        pl.pallas_call(
            split,
            out_shape=(jax.ShapeDtypeStruct(shape, f32), jax.ShapeDtypeStruct((3,) + shape, f32)),
            in_specs=[pl.BlockSpec(memory_space=pltpu.VMEM)],
            out_specs=(pl.BlockSpec(memory_space=pl.ANY), pl.BlockSpec(memory_space=pl.ANY)),
            scratch_shapes=[dma((2,))],
            compiler_params=pltpu.CompilerParams(vmem_limit_bytes=32 << 20),
        )(both)
    )


def solution(mesh):
    return jax.shard_map(
        local,
        mesh=mesh,
        in_specs=(P("gx", "gy", "gz"), P(None, "gx", "gy", "gz"), P("gx", "gy", "gz")),
        out_specs=(P("gx", "gy", "gz"), P(None, "gx", "gy", "gz")),
        check_vma=False,
    )
```

time: 28 us -> 26.9 us (0.961)
  Pallas kernels: 27.1 us -> 26.1 us
    pallas_call x1, Pallas kernels: 26.4 us -> 25.4 us  [local(): pl.pallas_call(kernel, out_shape=jax.ShapeDtypeStruct((4,) + shape, f32),...]
where the time goes in v4:
time: 26.9 us; the launch traced here: 26.7 us
  Pallas kernels  26.1 us (97%)
  between operations  0.64 us (2%)
    pallas_call x1, Pallas kernels, local(): pl.pallas_call(kernel, out_shape=jax.ShapeDtypeStruct((4,) + shape, f32),...  25.4 us
    pallas_call x1, Pallas kernels, local(): pl.pallas_call(split, out_shape=(jax.ShapeDtypeStruct(shape, f32), jax.Sh...  0.72 us

profile of v4, /device:TPU:0, one launch (start us, length us, event | category | flops | bytes accessed | tf_op | source)
XLA Modules:
  0.0 26.7 jit_solution(13467538523187338801)
XLA Ops:
  0.6 25.4 %shard_map.50.both = f32[4,4,32,128]{3,2,1,0:T(8,128)S(1)} custom-call(f32[4,32,128]{2,1,0:T(8,128)} %density.1, f32[3,4,32,128]{3,2,1,0:T(8,128)} %velocity.1, s32[4,32,128]{2,1,0:T(8,128)} %mask.1), custom_call_target="tpu_custom_call" | custom-call | tf_op jit(solution)/shard_map/pallas_call | solution.py:382
  26.0 0.7 %shard_map.51 = (f32[4,32,128]{2,1,0:T(8,128)}, f32[3,4,32,128]{3,2,1,0:T(8,128)}) custom-call(f32[4,4,32,128]{3,2,1,0:T(8,128)S(1)} %shard_map.50.both), custom_call_target="tpu_custom_call" | custom-call | tf_op jit(solution)/shard_map/pallas_call | solution.py:412

commit v5 on v4

--- a/solution.py
+++ b/solution.py
@@ -179,8 +179,8 @@
 
     def parts(start, slot):
         layers = pl.ds(start, 4)
-        refs = [fld.at[f, layers, 8:40] for f in range(3)]
-        refs += [fld.at[3, layers, 4:44], msk.at[pl.ds(start, 2), 4:44], msk.at[pl.ds(start + 2, 2), 4:44]]
+        refs = [fld.at[f, layers, 8:40] for f in range(3)] + [fld.at[f, layers, 4:44] for f in range(3, 4)]
+        refs += [msk.at[pl.ds(start, 2), 4:44], msk.at[pl.ds(start + 2, 2), 4:44]]
         refs += [peer.at[slot]]
         return refs
 
@@ -275,16 +275,22 @@
         unroll = 2
 
         def body(i, carry):
-            for k in range(unroll):
-                x = start + unroll * i + k
-                store_side(side_to, x, collide(pull_side(side, x), gmsk[x] > 0.5))
-            for k in range(unroll):
-                x = start + unroll * i + k
-                for b, r in enumerate(BLOCKS):
-                    rows = slice(r, r + 8)
-                    out = collide(pull_main(main, side, x, b), msk[x, rows] == 1)
-                    for q in range(19):
-                        main_to[q, x, rows] = out[q]
+            x = start + 2 * i + 0
+            store_side(side_to, x, collide(pull_side(side, x), gmsk[x] > 0.5))
+            x = start + 2 * i + 0
+            for b, r in [(b, BLOCKS[b]) for b in [0, 1, 2, 3, 4]]:
+                rows = slice(r, r + 8)
+                out = collide(pull_main(main, side, x, b), msk[x, rows] == 1)
+                for q in range(19):
+                    main_to[q, x, rows] = out[q]
+            x = start + 2 * i + 1
+            for b, r in [(b, BLOCKS[b]) for b in [0, 1, 2, 3, 4]]:
+                rows = slice(r, r + 8)
+                out = collide(pull_main(main, side, x, b), msk[x, rows] == 1)
+                for q in range(19):
+                    main_to[q, x, rows] = out[q]
+            x = start + 2 * i + 1
+            store_side(side_to, x, collide(pull_side(side, x), gmsk[x] > 0.5))
             return carry
 
         lax.fori_loop(0, count // unroll, body, 0)
@@ -294,22 +300,28 @@
     for c in x_copies[3:6]:
         c.start()
     first_four(4)
-    for i in range(3):
-        x_copies[i].wait_recv()
-        f_copies[i].start()
+    x_copies[0].wait_recv()
+    f_copies[0].start()
+    x_copies[1].wait_recv()
+    f_copies[1].start()
+    x_copies[2].wait_recv()
+    f_copies[2].start()
     for c in e_copies[:2]:
         c.start()
     z_copy.wait_recv()
     x_copies[6].start()
     x_copies[3].wait_recv()
     f_copies[3].start()
-    for i in range(4, 7):
-        x_copies[i].wait_recv()
-        f_copies[i].start()
+    x_copies[4].wait_recv()
+    f_copies[4].start()
     for c in f_copies[:3]:
         c.wait_recv()
     for c in e_copies[2:]:
         c.start()
+    x_copies[5].wait_recv()
+    f_copies[5].start()
+    x_copies[6].wait_recv()
+    f_copies[6].start()
     for c in e_copies[:2]:
         c.wait_recv()
 
@@ -320,9 +332,10 @@
     step_layers(3, 6 - 4 * par, 4)
     step_layers(4, 7 - 4 * par, 2)
 
-    for c in f_copies[3:] + e_copies[2:]:
+    for c in f_copies[3:6] + e_copies[2:]:
         c.wait_recv()
     first_four(8 * par)
+    f_copies[6].wait_recv()
     first_side(8 * par, far_slot)
     step_layers(2, 1 + 6 * par, 4)
     step_layers(3, 2 + 4 * par, 4)

time: 26.9 us -> 26.5 us (0.985)
  Pallas kernels: 26.1 us -> 25.7 us
    pallas_call x1, Pallas kernels: 25.4 us -> 25 us  [local(): pl.pallas_call(kernel, out_shape=jax.ShapeDtypeStruct((4,) + shape, f32),...]
where the time goes in v5:
time: 26.5 us; the launch traced here: 26.4 us
  Pallas kernels  25.7 us (97%)
  between operations  0.64 us (2%)
    pallas_call x1, Pallas kernels, local(): pl.pallas_call(kernel, out_shape=jax.ShapeDtypeStruct((4,) + shape, f32),...  25 us
    pallas_call x1, Pallas kernels, local(): pl.pallas_call(split, out_shape=(jax.ShapeDtypeStruct(shape, f32), jax.Sh...  0.72 us

profile of v5, /device:TPU:0, one launch (start us, length us, event | category | flops | bytes accessed | tf_op | source)
XLA Modules:
  0.0 26.4 jit_solution(12005125945553846075)
XLA Ops:
  0.6 25.0 %shard_map.50.both = f32[4,4,32,128]{3,2,1,0:T(8,128)S(1)} custom-call(f32[4,32,128]{2,1,0:T(8,128)} %density.1, f32[3,4,32,128]{3,2,1,0:T(8,128)} %velocity.1, s32[4,32,128]{2,1,0:T(8,128)} %mask.1), custom_call_target="tpu_custom_call" | custom-call | tf_op jit(solution)/shard_map/pallas_call | solution.py:395
  25.7 0.7 %shard_map.51 = (f32[4,32,128]{2,1,0:T(8,128)}, f32[3,4,32,128]{3,2,1,0:T(8,128)}) custom-call(f32[4,4,32,128]{3,2,1,0:T(8,128)S(1)} %shard_map.50.both), custom_call_target="tpu_custom_call" | custom-call | tf_op jit(solution)/shard_map/pallas_call | solution.py:425

commit v6 on v5

--- a/solution.py
+++ b/solution.py
@@ -33,7 +33,7 @@
 
 LAYERS, ROWS, LANES = 12, 48, 128
 BLOCKS = [4 + 8 * j for j in range(5)]
-SIDE = 4
+SIDE = 8
 
 
 def moments(f):
@@ -366,9 +366,8 @@
             for b, r in enumerate(BLOCKS):
                 rest, up, down = pull(main_b, x, r, 0), moved(x, b, 1), moved(x, b, -1)
                 rho, mx, my = (rest[k] + (up[k] + down[k]) for k in range(3))
-                low, high = max(r, 8), min(r + 8, 40)
                 for k, value in enumerate((rho, mx, my, up[0] - down[0])):
-                    out[k, x - 4, low - 8 : high - 8] = value[low - r : high - r]
+                    out[k, x - 4, r : r + 8] = value
         return carry
 
     lax.fori_loop(0, 4 // 4, last, 0)
@@ -379,8 +378,8 @@
 
 def split(both, density, momentum, sem):
     copies = [
-        pltpu.make_async_copy(both.at[0], density, sem.at[0]),
-        pltpu.make_async_copy(both.at[1:4], momentum, sem.at[1]),
+        pltpu.make_async_copy(both.at[0, :, 8:40], density, sem.at[0]),
+        pltpu.make_async_copy(both.at[1:4, :, 8:40], momentum, sem.at[1]),
     ]
     for c in copies:
         c.start()
@@ -394,7 +393,7 @@
     dma = pltpu.SemaphoreType.DMA
     both = pl.pallas_call(
             kernel,
-            out_shape=jax.ShapeDtypeStruct((4,) + shape, f32),
+            out_shape=jax.ShapeDtypeStruct((4, shape[0], ROWS, LANES), f32),
             in_specs=[pl.BlockSpec(memory_space=pl.ANY)] * 3,
             out_specs=pl.BlockSpec(memory_space=pltpu.VMEM),
             scratch_shapes=[
@@ -405,8 +404,8 @@
                 pltpu.VMEM((LAYERS, 8, LANES), f32),
                 pltpu.VMEM((19, LAYERS, ROWS, LANES), f32),
                 pltpu.VMEM((19, LAYERS, ROWS, LANES), f32),
-                pltpu.VMEM((19, LAYERS, 16, LANES), f32),
-                pltpu.VMEM((19, LAYERS, 16, LANES), f32),
+                pltpu.VMEM((19, LAYERS, 24, LANES), f32),
+                pltpu.VMEM((19, LAYERS, 24, LANES), f32),
                 dma((3,)),
                 dma((4,)),
                 dma((4,)),

time: 26.5 us -> 26.5 us (level)
  no operation moved by 1% of the time
where the time goes in v6:
time: 26.5 us; the launch traced here: 26.4 us
  Pallas kernels  25.8 us (97%)
  between operations  0.64 us (2%)
    pallas_call x1, Pallas kernels, local(): pl.pallas_call(kernel, out_shape=jax.ShapeDtypeStruct((4, shape[0], ROWS,...  25.1 us
    pallas_call x1, Pallas kernels, local(): pl.pallas_call(split, out_shape=(jax.ShapeDtypeStruct(shape, f32), jax.Sh...  0.72 us

profile of v6, /device:TPU:0, one launch (start us, length us, event | category | flops | bytes accessed | tf_op | source)
XLA Modules:
  0.0 26.4 jit_solution(3124997148997005451)
XLA Ops:
  0.6 25.1 %shard_map.50.both = f32[4,4,48,128]{3,2,1,0:T(8,128)S(1)} custom-call(f32[4,32,128]{2,1,0:T(8,128)} %density.1, f32[3,4,32,128]{3,2,1,0:T(8,128)} %velocity.1, s32[4,32,128]{2,1,0:T(8,128)} %mask.1), custom_call_target="tpu_custom_call" | custom-call | tf_op jit(solution)/shard_map/pallas_call | solution.py:394
  25.7 0.7 %shard_map.51 = (f32[4,32,128]{2,1,0:T(8,128)}, f32[3,4,32,128]{3,2,1,0:T(8,128)}) custom-call(f32[4,4,48,128]{3,2,1,0:T(8,128)S(1)} %shard_map.50.both), custom_call_target="tpu_custom_call" | custom-call | tf_op jit(solution)/shard_map/pallas_call | solution.py:424

commit v7 on v6

--- a/solution.py
+++ b/solution.py
@@ -310,6 +310,7 @@
         c.start()
     z_copy.wait_recv()
     x_copies[6].start()
+    first_side(4, 1)
     x_copies[3].wait_recv()
     f_copies[3].start()
     x_copies[4].wait_recv()
@@ -325,7 +326,6 @@
     for c in e_copies[:2]:
         c.wait_recv()
 
-    first_side(4, 1)
     first_four(8 - 8 * par)
     first_side(8 - 8 * par, near_slot)
     step_layers(2, 5 - 4 * par, 6)

time: 26.5 us -> 26.5 us (level)
  no operation moved by 1% of the time
where the time goes in v7:
time: 26.5 us; the launch traced here: 26.4 us
  Pallas kernels  25.8 us (97%)
  between operations  0.64 us (2%)
    pallas_call x1, Pallas kernels, local(): pl.pallas_call(kernel, out_shape=jax.ShapeDtypeStruct((4, shape[0], ROWS,...  25.1 us
    pallas_call x1, Pallas kernels, local(): pl.pallas_call(split, out_shape=(jax.ShapeDtypeStruct(shape, f32), jax.Sh...  0.72 us

profile of v7, /device:TPU:0, one launch (start us, length us, event | category | flops | bytes accessed | tf_op | source)
XLA Modules:
  0.0 26.4 jit_solution(10410558081362820729)
XLA Ops:
  0.6 25.1 %shard_map.50.both = f32[4,4,48,128]{3,2,1,0:T(8,128)S(1)} custom-call(f32[4,32,128]{2,1,0:T(8,128)} %density.1, f32[3,4,32,128]{3,2,1,0:T(8,128)} %velocity.1, s32[4,32,128]{2,1,0:T(8,128)} %mask.1), custom_call_target="tpu_custom_call" | custom-call | tf_op jit(solution)/shard_map/pallas_call | solution.py:394
  25.7 0.7 %shard_map.51 = (f32[4,32,128]{2,1,0:T(8,128)}, f32[3,4,32,128]{3,2,1,0:T(8,128)}) custom-call(f32[4,4,48,128]{3,2,1,0:T(8,128)S(1)} %shard_map.50.both), custom_call_target="tpu_custom_call" | custom-call | tf_op jit(solution)/shard_map/pallas_call | solution.py:424

commit v8 on v6

--- a/solution.py
+++ b/solution.py
@@ -103,6 +103,7 @@
     msk,
     pack,
     peer,
+    cols,
     gmsk,
     main_a,
     main_b,
@@ -207,6 +208,7 @@
         acc = None
         for k, m in enumerate(range(3 * v, min(3 * v + 3, 20))):
             part = columns(m // 4, 4 + m % 4)
+            cols[1, m] = part
             part = pltpu.roll(part, 40 * k, 1) if k else part
             acc = part if acc is None else jnp.where(group >= 5 * k, part, acc)
         pack[v] = acc
@@ -231,13 +233,17 @@
             elif cy == -1:
                 side[q, x, SIDE + 8 : SIDE + 9] = pltpu.roll(out[q], LANES - 8, 1)[0:1]
 
+    def side_columns(start, slot):
+        for m in range(20):
+            cols[slot, m] = columns(m // 4, start + m % 4)
+
     def first_side(start, slot):
         for i in range(4):
             x = start + i
             cells = []
             for f in range(5):
                 m = 4 * f + i
-                mine = columns(f, x)
+                mine = cols[slot, m]
                 theirs = peer[slot, m // 3]
                 theirs = pltpu.roll(theirs, LANES - 40 * (m % 3), 1) if m % 3 else theirs
                 above = pltpu.roll(jnp.where(low_half, mine, theirs), 64, 1)
@@ -327,6 +333,7 @@
 
     first_side(4, 1)
     first_four(8 - 8 * par)
+    side_columns(8 - 8 * par, near_slot)
     first_side(8 - 8 * par, near_slot)
     step_layers(2, 5 - 4 * par, 6)
     step_layers(3, 6 - 4 * par, 4)
@@ -335,6 +342,7 @@
     for c in f_copies[3:6] + e_copies[2:]:
         c.wait_recv()
     first_four(8 * par)
+    side_columns(8 * par, far_slot)
     f_copies[6].wait_recv()
     first_side(8 * par, far_slot)
     step_layers(2, 1 + 6 * par, 4)
@@ -401,6 +409,7 @@
                 pltpu.VMEM((LAYERS, ROWS, LANES), jnp.int32),
                 pltpu.VMEM((7, 8, LANES), f32),
                 pltpu.VMEM((3, 7, 8, LANES), f32),
+                pltpu.VMEM((3, 20, 8, LANES), f32),
                 pltpu.VMEM((LAYERS, 8, LANES), f32),
                 pltpu.VMEM((19, LAYERS, ROWS, LANES), f32),
                 pltpu.VMEM((19, LAYERS, ROWS, LANES), f32),

time: 26.5 us -> 26.5 us (level)
  no operation moved by 1% of the time
where the time goes in v8:
time: 26.5 us; the launch traced here: 26.4 us
  Pallas kernels  25.8 us (97%)
  between operations  0.64 us (2%)
    pallas_call x1, Pallas kernels, local(): pl.pallas_call(kernel, out_shape=jax.ShapeDtypeStruct((4, shape[0], ROWS,...  25 us
    pallas_call x1, Pallas kernels, local(): pl.pallas_call(split, out_shape=(jax.ShapeDtypeStruct(shape, f32), jax.Sh...  0.72 us

profile of v8, /device:TPU:0, one launch (start us, length us, event | category | flops | bytes accessed | tf_op | source)
XLA Modules:
  0.0 26.4 jit_solution(130149607317338214)
XLA Ops:
  0.6 25.0 %shard_map.50.both = f32[4,4,48,128]{3,2,1,0:T(8,128)S(1)} custom-call(f32[4,32,128]{2,1,0:T(8,128)} %density.1, f32[3,4,32,128]{3,2,1,0:T(8,128)} %velocity.1, s32[4,32,128]{2,1,0:T(8,128)} %mask.1), custom_call_target="tpu_custom_call" | custom-call | tf_op jit(solution)/shard_map/pallas_call | solution.py:402
  25.7 0.7 %shard_map.51 = (f32[4,32,128]{2,1,0:T(8,128)}, f32[3,4,32,128]{3,2,1,0:T(8,128)}) custom-call(f32[4,4,48,128]{3,2,1,0:T(8,128)S(1)} %shard_map.50.both), custom_call_target="tpu_custom_call" | custom-call | tf_op jit(solution)/shard_map/pallas_call | solution.py:433
